TPU v7x, 32 devices: a whole 2x2x4 slice. The times are simulated.
32 devices in a mesh: fy: 2 (over x), fx: 8 (over z, y), ch: 2 (over core).
Axes of the slice: x: 2, y: 2, z: 4, core: 2. Of those that a mesh axis runs over, the one named last changes fastest.
Arguments:
- image_cube: float32 [64, 512, 416], P('ch', 'fx', 'fy'), may hold values from 0 to 2
- data_grad: bfloat16 [64, 512, 416], P('ch', 'fx', 'fy'), may hold values from -6 to 6
- dual_coeffs: float32 [64, 896, 512], P('ch', 'fx', 'fy'), may hold values from -6 to 6
- reweights: float32 [896, 512], P('fx', 'fy'), may hold values from 1 to 40
Outputs:
- image_next: float32 [64, 512, 416], P('ch', 'fx', 'fy')
- dual_next: float32 [64, 896, 512], P('ch', 'fx', 'fy')
All inputs are finite; a program needn't handle non-finite values.
Results may differ from a plain program's by a relative error of at most 0.0003.
Values sent between devices are 32-bit elements; how exact they have to be, the bound alone decides.
A program may use at most 64 MiB of HBM per device.

v0:
```python
import functools

import jax
import jax.numpy as jnp
import numpy as np
from jax import lax
from jax.experimental import pallas as pl
from jax.experimental.pallas import tpu as pltpu
from jax.sharding import PartitionSpec as P

LEVELS = 2
LOW_PASS = [
    -0.00011747678400228192,
    0.0006754494059985568,
    -0.0003917403729959771,
    -0.00487035299301066,
    0.008746094047015655,
    0.013981027917015516,
    -0.04408825393106472,
    -0.01736930100202211,
    0.128747426620186,
    0.00047248457399797254,
    -0.2840155429624281,
    -0.015829105256023893,
    0.5853546836548691,
    0.6756307362980128,
    0.3128715909144659,
    0.05441584224308161,
]
TAU_STEP = 0.5
LAMBDA_REG = 1.0
EPSILON = 1e-06
LANES = 128
CHUNK = 2
AT_B, AT_VIA_L, AT_C, AT_VIA_R, AT_D, AT_E = 1, 3, 4, 6, 7, 9
MESH = pl.DeviceIdType.MESH
F32 = jnp.float32
BF16 = jnp.bfloat16


def level_matrix(length):
    halved = length // 2
    taps_count = len(LOW_PASS)
    matrix = np.zeros((length, length))
    for out_row in range(halved):
        for tap_index in range(taps_count):
            column = (2 * out_row + tap_index) % length
            matrix[out_row, column] += LOW_PASS[tap_index]
            matrix[halved + out_row, column] += (-1) ** tap_index * LOW_PASS[
                taps_count - 1 - tap_index
            ]
    return matrix


def halves(matrix):
    exact = np.asarray(matrix, np.float32)
    high = exact.astype(BF16)
    low = (exact - high.astype(np.float32)).astype(BF16)
    return high, low


def right_factor(matrix):
    high, low = halves(matrix)
    return jnp.asarray(np.concatenate([high, low, high], axis=0))


def left_factor(matrix, padded):
    high, low = halves(np.pad(matrix, ((0, 0), (0, padded - matrix.shape[1]))))
    return jnp.asarray(np.concatenate([high, low, high], axis=1))


def round_up(value, to):
    return -(-value // to) * to


def split(x):
    high = x.astype(BF16)
    low = (x - high.astype(F32)).astype(BF16)
    return high, low


def times_right(x, factor):
    n, rows, columns = x.shape
    high, low = split(x.reshape(n * rows, columns))
    out = jnp.dot(jnp.concatenate([high, high, low], axis=1), factor, preferred_element_type=F32)
    return out.reshape(n, rows, out.shape[1])


def times_left(factor, x):
    rows = x.shape[0]
    padded = round_up(rows, 16)
    if padded > rows:
        x = jnp.concatenate([x, jnp.zeros((padded - rows, x.shape[1]), F32)], axis=0)
    high, low = split(x)
    return jnp.dot(factor, jnp.concatenate([high, high, low], axis=0), preferred_element_type=F32)


def corner_step(corner, right, left):
    n = corner.shape[0]
    width = corner.shape[2]
    mid = times_right(corner, right)
    pieces = []
    for c in range(0, n, 2):
        pair = times_left(left, jnp.concatenate([mid[c], mid[c + 1]], axis=1))
        pieces += [pair[:, :width], pair[:, width:]]
    return pieces


def kernel(
    names,
    image_hbm, grad_hbm, dual_hbm, rew_ref,
    sy0_ref, sx0_ref, sy1_ref, sx1_ref, ay0_ref, ax0_ref, ay1_ref, ax1_ref,
    next_hbm, upd_hbm, factor_ref,
    image, grad, dual, work, y1s, y1r, ls, lr, rs, rr, y2s, y2r, via, acc, accr,
    in_sem, out_sem, send_sem, recv_sem, via_send, via_recv, ch_send, ch_recv,
):
    fy_name, fx_name, ch_name = names
    channels, tx, ty = image.shape
    ex, ey = dual.shape[1:]
    border = ex - tx
    n = CHUNK
    chunks = channels // n
    half = ex // 2
    tail = ty - LANES
    fy, fx, ch = (lax.axis_index(a) for a in names)
    n_fy, n_fx, n_ch = (lax.axis_size(a) for a in names)
    has_up, has_down = fy > 0, fy < n_fy - 1
    has_left, has_right = fx > 0, fx < n_fx - 1

    barrier = pltpu.get_barrier_semaphore()
    near = (
        (has_up, {fy_name: fy - 1}),
        (has_down, {fy_name: fy + 1}),
        (has_left, {fx_name: fx - 1}),
        (has_right, {fx_name: fx + 1}),
        (fx > 1, {fx_name: fx - 2}),
        (fx < n_fx - 2, {fx_name: fx + 2}),
    )
    for there, where in near:
        @pl.when(there)
        def _(where=where):
            pl.semaphore_signal(barrier, inc=1, device_id=where, device_id_type=MESH)
    for step in range(1, n_ch):
        pl.semaphore_signal(
            barrier, inc=1, device_id={ch_name: lax.rem(ch + step, n_ch)}, device_id_type=MESH
        )

    def part(k):
        return pl.ds(k * n, n)

    def load(k, which):
        src, dst = ((dual_hbm, dual), (image_hbm, image), (grad_hbm, grad))[which]
        return pltpu.make_async_copy(src.at[part(k)], dst.at[part(k)], in_sem.at[which, k])

    def store(k, which):
        src, dst = ((image, next_hbm), (dual, upd_hbm))[which]
        return pltpu.make_async_copy(src.at[part(k)], dst.at[part(k)], out_sem.at[which, k])

    links = (
        (y1s, y1r, {fy_name: fy - 1}),
        (ls, lr, {fx_name: fx - 1}),
        (rs, rr, {fx_name: fx + 1}),
        (y2s, y2r, {fy_name: fy + 1}),
    )

    def link(k, which):
        src, dst, where = links[which]
        return pltpu.make_async_remote_copy(
            src_ref=src.at[part(k)],
            dst_ref=dst.at[part(k)],
            send_sem=send_sem.at[which, k],
            recv_sem=recv_sem.at[which, k],
            device_id=where,
            device_id_type=MESH,
        )

    odd = lax.rem(fx, 2) == 1
    groups = n_fx // 2

    def turn(k, m):
        return ((k + 1) * m) // groups - (k * m) // groups == 1

    def sends_via(k, which):
        if which == 1:
            return jnp.logical_not(odd) & has_left & has_right & turn(k, fx // 2)
        return odd & has_left & has_right & jnp.logical_not(turn(k, (fx + 1) // 2))

    def to_via(k, which):
        return pltpu.make_async_remote_copy(
            src_ref=links[which][0].at[part(k)],
            dst_ref=via.at[part(k)],
            send_sem=send_sem.at[which, k],
            recv_sem=via_recv.at[k],
            device_id={fx_name: fx + 1 if which == 1 else fx - 1},
            device_id_type=MESH,
        )

    def passes_on(k, which):
        if which == 1:
            return odd & (fx > 2) & turn(k, fx // 2)
        return jnp.logical_not(odd) & (fx < n_fx - 2) & jnp.logical_not(turn(k, (fx + 2) // 2))

    def from_via(k, which):
        return pltpu.make_async_remote_copy(
            src_ref=via.at[part(k)],
            dst_ref=links[which][1].at[part(k)],
            send_sem=via_send.at[k],
            recv_sem=recv_sem.at[which, k],
            device_id={fx_name: fx - 2 if which == 1 else fx + 2},
            device_id_type=MESH,
        )

    def stage_via(which, k):
        @pl.when(passes_on(k, which))
        def _():
            to_via(k, which).wait_recv()
            from_via(k, which).start()

    def loads(k, carry):
        load(k, 0).start()
        return carry

    def more_loads(k, carry):
        load(k, 1).start()
        load(k, 2).start()
        return carry

    lax.fori_loop(0, chunks, loads, 0)
    lax.fori_loop(0, chunks, more_loads, 0)
    acc[...] = jnp.zeros_like(acc)

    peers = n_ch - 1
    for at, size in ((fy, n_fy), (fx, n_fx)):
        peers = peers + jnp.minimum(at, 1) + jnp.minimum(size - 1 - at, 1)
    peers = peers + jnp.minimum(fx // 2, 1) + jnp.minimum((n_fx - 1 - fx) // 2, 1)
    pl.semaphore_wait(barrier, peers)

    def lanes(rows):
        return lax.broadcasted_iota(jnp.int32, (rows, LANES), 1)

    def own_edge(rows):
        at = lanes(rows)
        return (at >= tail - border) & (at < tail)

    def roll(x, by):
        return pltpu.roll(x, by % LANES, 1)

    def send_borders(k, which, buffer):
        def one(c):
            main = work[c, (0 if which == 1 else ex - border):(border if which == 1 else ex), :LANES]
            rest = work[c, (0 if which == 1 else ex - border):(border if which == 1 else ex), LANES:]
            g = border // 3
            a, b, d = rest[:g], rest[g:2 * g], rest[2 * g:]
            low = lanes(g) < tail
            buffer[c, :border] = main
            buffer[c, border:border + g] = jnp.where(low, a, roll(b, tail))
            buffer[c, border + g:] = jnp.where(low, d, roll(b, 2 * tail - LANES))
        for j in range(n):
            one(k * n + j)
        around = sends_via(k, which)

        @pl.when(around)
        def _():
            to_via(k, which).start()

        @pl.when(jnp.logical_not(around))
        def _():
            link(k, which).start()

    def unpacked(buffer, c):
        g = border // 3
        p, q = buffer[c, border:border + g], buffer[c, border + g:]
        b = jnp.where(lanes(g) < LANES - tail, roll(p, -tail), roll(q, LANES - 2 * tail))
        return buffer[c, :border], jnp.concatenate([p, b, q], axis=0)

    def stage_a(k):
        load(k, 0).wait()
        x = dual[part(k)]
        hx, hy = ex // 2, ey // 2
        corner = corner_step(x[:, :hx, :hy], sy1_ref[...], sx1_ref[...])
        full = jnp.stack(
            [
                jnp.concatenate(
                    [jnp.concatenate([corner[j], x[j, :hx, hy:]], axis=1), x[j, hx:]], axis=0
                )
                for j in range(n)
            ]
        )
        mid = times_right(full, sy0_ref[...])
        for j in range(n):
            work[k * n + j] = times_left(sx0_ref[...], mid[j])

        @pl.when(has_up)
        def _():
            edge = own_edge(half)
            for j in range(n):
                c = k * n + j
                first, second = work[c, :half, LANES:], work[c, half:, LANES:]
                y1s[c] = jnp.where(edge, roll(first, -border), roll(second, half_lane - border))
            link(k, 0).start()

    half_lane = LANES // 2

    def stage_b(k):
        @pl.when(has_down)
        def _():
            link(k, 0).wait_recv()
            edge = own_edge(half)
            for j in range(n):
                c = k * n + j
                got = y1r[c]
                work[c, :half, LANES:] += jnp.where(edge, got, 0.0)
                work[c, half:, LANES:] += jnp.where(edge, roll(got, half_lane), 0.0)

        @pl.when(has_left)
        def _():
            send_borders(k, 1, ls)

    def stage_c(k):
        @pl.when(has_right)
        def _():
            link(k, 1).wait_recv()
            for j in range(n):
                c = k * n + j
                main, rest = unpacked(lr, c)
                work[c, ex - border:, :LANES] += main
                work[c, ex - border:, LANES:] += rest

        load(k, 1).wait()
        load(k, 2).wait()
        xs = lax.broadcasted_iota(jnp.int32, (tx, ty), 0)
        ys = lax.broadcasted_iota(jnp.int32, (tx, ty), 1)
        ax = jnp.where((xs >= tx - border) & has_right, 0.5**0.5, 1.0).astype(F32)
        by = jnp.where((ys >= ty - border) & has_down, 0.5**0.5, 1.0).astype(F32)
        weight = ax * by
        for j in range(n):
            c = k * n + j
            adjoint = work[c, border:, :ty] * weight
            current = image[c]
            fresh = jnp.maximum(current - TAU_STEP * (grad[c].astype(F32) + adjoint), 0.0)
            work[c, border:, :ty] = (2.0 * fresh - current) * weight
            image[c] = fresh
        store(k, 0).start()

        @pl.when(has_right)
        def _():
            send_borders(k, 2, rs)

    def stage_d(k):
        @pl.when(has_left)
        def _():
            link(k, 2).wait_recv()
            for j in range(n):
                c = k * n + j
                main, rest = unpacked(rr, c)
                work[c, :border, :LANES] = main
                work[c, :border, LANES:] = rest

        @pl.when(jnp.logical_not(has_left))
        def _():
            for j in range(n):
                work[k * n + j, :border] = jnp.zeros((border, ey), F32)

        @pl.when(has_down)
        def _():
            edge = own_edge(half)
            for j in range(n):
                c = k * n + j
                y2s[c] = jnp.where(edge, work[c, :half, LANES:], roll(work[c, half:, LANES:], half_lane))
            link(k, 3).start()

    def stage_e(k):
        @pl.when(has_up)
        def _():
            link(k, 3).wait_recv()
            low = lanes(half) < tail
            for j in range(n):
                c = k * n + j
                got = y2r[c]
                work[c, :half, LANES:] = jnp.where(low, work[c, :half, LANES:], roll(got, border))
                work[c, half:, LANES:] = jnp.where(low, work[c, half:, LANES:], roll(got, border - half_lane))

        @pl.when(jnp.logical_not(has_up))
        def _():
            low = lanes(ex) < tail
            for j in range(n):
                c = k * n + j
                work[c, :, LANES:] = jnp.where(low, work[c, :, LANES:], 0.0)

        mid = times_right(work[part(k)], ay0_ref[...])
        hx, hy = ex // 2, ey // 2
        full = [times_left(ax0_ref[...], mid[j]) for j in range(n)]
        corner = corner_step(jnp.stack([f[:hx, :hy] for f in full]), ay1_ref[...], ax1_ref[...])
        total = acc[...]
        for j in range(n):
            c = k * n + j
            coeffs = jnp.concatenate(
                [jnp.concatenate([corner[j], full[j][:hx, hy:]], axis=1), full[j][hx:]], axis=0
            )
            updated = dual[c] + coeffs
            total = total + updated * updated
            dual[c] = updated
        acc[...] = total
        store(k, 1).start()

    stages = (
        (0, stage_a),
        (AT_B, stage_b),
        (AT_VIA_L, functools.partial(stage_via, 1)),
        (AT_C, stage_c),
        (AT_VIA_R, functools.partial(stage_via, 2)),
        (AT_D, stage_d),
        (AT_E, stage_e),
    )

    def step(t, carry):
        for delay, stage in stages:
            @pl.when((t >= delay) & (t < chunks + delay))
            def _(delay=delay, stage=stage):
                stage(t - delay)
        return carry

    lax.fori_loop(0, chunks + AT_E, step, 0)

    def across(step):
        return pltpu.make_async_remote_copy(
            src_ref=acc,
            dst_ref=accr.at[step - 1],
            send_sem=ch_send.at[step - 1],
            recv_sem=ch_recv.at[step - 1],
            device_id={ch_name: lax.rem(ch + step, n_ch)},
            device_id_type=MESH,
        )

    for s in range(1, n_ch):
        across(s).start()

    def drain(k, carry):
        for which, there in ((0, has_up), (1, has_left), (2, has_right), (3, has_down)):
            @pl.when(there)
            def _(which=which):
                link(k, which).wait_send()
        for which in (1, 2):
            @pl.when(passes_on(k, which))
            def _(which=which):
                from_via(k, which).wait_send()
        store(k, 0).wait()
        store(k, 1).wait()
        return carry

    lax.fori_loop(0, chunks, drain, 0)
    for s in range(1, n_ch):
        across(s).wait()
    total = acc[...]
    for s in range(1, n_ch):
        total = total + accr[s - 1]
    factor_ref[...] = jnp.minimum(1.0, LAMBDA_REG * rew_ref[...] / jnp.sqrt(total + EPSILON))


def shards(names, image_cube, data_grad, dual_coeffs, reweights):
    channels, tx, ty = image_cube.shape
    _, ex, ey = dual_coeffs.shape
    border = ex - tx
    n_ch = lax.axis_size(names[2])
    chunks = channels // CHUNK
    packed = border + 2 * (border // 3)
    wy0 = np.roll(level_matrix(ey), -(ey - ty), axis=1)
    wx0 = level_matrix(ex)
    wy1, wx1 = level_matrix(ey // 2), level_matrix(ex // 2)
    px0, px1 = round_up(ex, 16), round_up(ex // 2, 16)
    factors = (
        right_factor(wy0), left_factor(wx0.T, px0), right_factor(wy1), left_factor(wx1.T, px1),
        right_factor(wy0.T), left_factor(wx0, px0), right_factor(wy1.T), left_factor(wx1, px1),
    )
    anywhere = pl.BlockSpec(memory_space=pl.ANY)
    inside = pl.BlockSpec(memory_space=pltpu.VMEM)
    lines = pltpu.VMEM((channels, ex // 2, LANES), F32)
    sides = pltpu.VMEM((channels, packed, LANES), F32)
    image_next, updated, factor = pl.pallas_call(
        functools.partial(kernel, names),
        out_shape=(
            jax.ShapeDtypeStruct((channels, tx, ty), F32),
            jax.ShapeDtypeStruct((channels, ex, ey), F32),
            jax.ShapeDtypeStruct((ex, ey), F32),
        ),
        in_specs=[pl.BlockSpec(memory_space=pltpu.HBM)] * 3 + [inside] * 9,
        out_specs=(anywhere, anywhere, inside),
        scratch_shapes=[
            pltpu.VMEM((channels, tx, ty), F32),
            pltpu.VMEM((channels, tx, ty), BF16),
            pltpu.VMEM((channels, ex, ey), F32),
            pltpu.VMEM((channels, ex, ey), F32),
            lines, lines, sides, sides, sides, sides, lines, lines, sides,
            pltpu.VMEM((ex, ey), F32),
            pltpu.VMEM((n_ch - 1, ex, ey), F32),
            pltpu.SemaphoreType.DMA((3, chunks)),
            pltpu.SemaphoreType.DMA((2, chunks)),
            pltpu.SemaphoreType.DMA((4, chunks)),
            pltpu.SemaphoreType.DMA((4, chunks)),
            pltpu.SemaphoreType.DMA((chunks,)),
            pltpu.SemaphoreType.DMA((chunks,)),
            pltpu.SemaphoreType.DMA((n_ch - 1,)),
            pltpu.SemaphoreType.DMA((n_ch - 1,)),
        ],
        compiler_params=pltpu.CompilerParams(
            collective_id=0, has_side_effects=True, vmem_limit_bytes=60 * 2**20
        ),
        name="facets",
    )(image_cube, data_grad, dual_coeffs, reweights, *factors)
    return image_next, updated * factor[None]


def solution(mesh):
    names = ("fy", "fx", "ch")
    return jax.shard_map(
        functools.partial(shards, names),
        mesh=mesh,
        in_specs=(P("ch", "fx", "fy"), P("ch", "fx", "fy"), P("ch", "fx", "fy"), P("fx", "fy")),
        out_specs=(P("ch", "fx", "fy"), P("ch", "fx", "fy")),
        check_vma=False,
    )
```

profile of v0, /device:TPU:19, one launch (start us, length us, event | category | flops | bytes accessed | tf_op | source)
XLA Modules:
  0.0 79.6 jit_solution(14666281367848893347)
XLA Ops:
  0.6 73.4 %facets.1 = (f32[32,64,208]{2,1,0:T(8,128)}, f32[32,112,256]{2,1,0:T(8,128)}, f32[112,256]{1,0:T(8,128)}) custom-call(f32[32,64,208]{2,1,0:T(8,128)} %image_hbm.1, bf16[32,64,208]{2,1,0:T(8,128)(2,1)} %grad_hbm.1, f32[32,112,256]{2,1,0:T(8,128)} %dual_hbm.1, f32[112,256]{1,0:T(8,128)} %rew_ref.1, bf16[768,256]{1,0:T(8,128)(2,1)} %constant.16.clone.sy0_ref, ...), custom_call_target="tpu_custom_call" | custom-call | tf_op jit(solution)/shard_map/facets/pallas_call | solution.py:479
  74.0 0.0 copy-start
  74.0 4.3 %broadcast_multiply_fusion = f32[32,112,256]{2,1,0:T(8,128)} fusion(f32[32,112,256]{2,1,0:T(8,128)} %get-tuple-element.6, f32[112,256]{1,0:T(8,128)} %get-tuple-element.7), kind=kLoop, calls=%fused_computation | loop fusion | flops 917504 | bytes 7454720 | tf_op jit(solution)/shard_map/mul | solution.py:510
  78.3 0.0 copy-done
  78.3 1.3 %copy.15 = f32[32,64,208]{2,1,0:T(8,128)} copy(f32[32,64,208]{2,1,0:T(8,128)S(1)} %copy-done) | data formatting | bytes 3407872
Async XLA Ops:
  74.0 4.3 %copy-start = (f32[32,64,208]{2,1,0:T(8,128)S(1)}, f32[32,64,208]{2,1,0:T(8,128)}, u32[]{:S(2)}) copy-start(f32[32,64,208]{2,1,0:T(8,128)} %get-tuple-element.10) | copy-start | bytes 5111812
where the time goes:
time: 79.8 us; the launch traced here: 79.6 us
  Pallas kernels  73.4 us (92%)
  other arithmetic  4.28 us (5%)
  local copies, waits for them, and re-layouts  1.32 us (2%)
    pallas_call x1, Pallas kernels, shards(): pl.pallas_call(functools.partial(kernel, names), out_shape=(jax.ShapeDtyp...  73.4 us
    mul x1, other arithmetic, shards(): return (image_next, updated * factor[None])  4.28 us

commit v1 on v0

v1 whole, which is shorter than its diff:
```python
import functools

import jax
import jax.numpy as jnp
import numpy as np
from jax import lax
from jax.experimental import pallas as pl
from jax.experimental.pallas import tpu as pltpu
from jax.sharding import PartitionSpec as P

LEVELS = 2
LOW_PASS = [
    -0.00011747678400228192,
    0.0006754494059985568,
    -0.0003917403729959771,
    -0.00487035299301066,
    0.008746094047015655,
    0.013981027917015516,
    -0.04408825393106472,
    -0.01736930100202211,
    0.128747426620186,
    0.00047248457399797254,
    -0.2840155429624281,
    -0.015829105256023893,
    0.5853546836548691,
    0.6756307362980128,
    0.3128715909144659,
    0.05441584224308161,
]
TAU_STEP = 0.5
LAMBDA_REG = 1.0
EPSILON = 1e-06
LANES = 128
CHUNK = 2
AT_B, AT_VIA_L, AT_C, AT_VIA_R, AT_D, AT_E = 1, 2, 3, 5, 6, 8
MESH = pl.DeviceIdType.MESH
F32 = jnp.float32
BF16 = jnp.bfloat16


def level_matrix(length):
    halved = length // 2
    taps_count = len(LOW_PASS)
    matrix = np.zeros((length, length))
    for out_row in range(halved):
        for tap_index in range(taps_count):
            column = (2 * out_row + tap_index) % length
            matrix[out_row, column] += LOW_PASS[tap_index]
            matrix[halved + out_row, column] += (-1) ** tap_index * LOW_PASS[
                taps_count - 1 - tap_index
            ]
    return matrix


def halves(matrix):
    exact = np.asarray(matrix, np.float32)
    high = exact.astype(BF16)
    low = (exact - high.astype(np.float32)).astype(BF16)
    return high, low


def right_factor(matrix):
    high, low = halves(matrix)
    return jnp.asarray(np.concatenate([high, low, high], axis=0))


def left_factor(matrix, padded):
    high, low = halves(np.pad(matrix, ((0, 0), (0, padded - matrix.shape[1]))))
    return jnp.asarray(np.concatenate([high, low, high], axis=1))


def round_up(value, to):
    return -(-value // to) * to


def split(x):
    high = x.astype(BF16)
    low = (x - high.astype(F32)).astype(BF16)
    return high, low


def times_right(x, factor):
    n, rows, columns = x.shape
    high, low = split(x.reshape(n * rows, columns))
    out = jnp.dot(jnp.concatenate([high, high, low], axis=1), factor, preferred_element_type=F32)
    return out.reshape(n, rows, out.shape[1])


def times_left(factor, x):
    rows = x.shape[0]
    padded = round_up(rows, 16)
    if padded > rows:
        x = jnp.concatenate([x, jnp.zeros((padded - rows, x.shape[1]), F32)], axis=0)
    high, low = split(x)
    return jnp.dot(factor, jnp.concatenate([high, high, low], axis=0), preferred_element_type=F32)


def corner_step(corner, right, left):
    n = corner.shape[0]
    width = corner.shape[2]
    mid = times_right(corner, right)
    pieces = []
    for c in range(0, n, 2):
        pair = times_left(left, jnp.concatenate([mid[c], mid[c + 1]], axis=1))
        pieces += [pair[:, :width], pair[:, width:]]
    return pieces


def kernel(
    names,
    image_hbm, grad_hbm, dual_hbm, rew_hbm,
    sy0_hbm, sx0_hbm, sy1_hbm, sx1_hbm, ay0_hbm, ax0_hbm, ay1_hbm, ax1_hbm,
    next_ref, upd_ref, factor_ref,
    sy0_ref, sx0_ref, sy1_ref, sx1_ref, ay0_ref, ax0_ref, ay1_ref, ax1_ref, rew_ref,
    image, grad, dual, work, y1s, y1r, ls, lr, rs, rr, y2s, y2r, via, acc, accr,
    in_sem, const_sem, send_sem, recv_sem, via_send, via_recv, ch_send, ch_recv,
):
    fy_name, fx_name, ch_name = names
    channels, tx, ty = image.shape
    ex, ey = dual.shape[1:]
    border = ex - tx
    n = CHUNK
    chunks = channels // n
    half = ex // 2
    tail = ty - LANES
    packed = ls.shape[1]
    fy, fx, ch = (lax.axis_index(a) for a in names)
    n_fy, n_fx, n_ch = (lax.axis_size(a) for a in names)
    has_up, has_down = fy > 0, fy < n_fy - 1
    has_left, has_right = fx > 0, fx < n_fx - 1

    barrier = pltpu.get_barrier_semaphore()
    near = (
        (has_up, {fy_name: fy - 1}),
        (has_down, {fy_name: fy + 1}),
        (has_left, {fx_name: fx - 1}),
        (has_right, {fx_name: fx + 1}),
        (fx > 1, {fx_name: fx - 2}),
        (fx < n_fx - 2, {fx_name: fx + 2}),
    )
    for there, where in near:
        @pl.when(there)
        def _(where=where):
            pl.semaphore_signal(barrier, inc=1, device_id=where, device_id_type=MESH)
    for step in range(1, n_ch):
        pl.semaphore_signal(
            barrier, inc=1, device_id={ch_name: lax.rem(ch + step, n_ch)}, device_id_type=MESH
        )

    def part(k):
        return pl.ds(k * n, n)

    def load(k, which):
        src, dst = ((dual_hbm, dual), (image_hbm, image), (grad_hbm, grad))[which]
        return pltpu.make_async_copy(src.at[part(k)], dst.at[part(k)], in_sem.at[which, k])

    constants = (
        (sy1_hbm, sy1_ref), (sx1_hbm, sx1_ref), (sy0_hbm, sy0_ref), (sx0_hbm, sx0_ref),
        (ay0_hbm, ay0_ref), (ax0_hbm, ax0_ref), (ay1_hbm, ay1_ref), (ax1_hbm, ax1_ref),
        (rew_hbm, rew_ref),
    )

    def constant(i):
        src, dst = constants[i]
        return pltpu.make_async_copy(src, dst, const_sem.at[i])

    whole, first_rows, last_rows = pl.ds(0, packed), pl.ds(0, border), pl.ds(border, packed - border)
    corner_half, own_half = border // 2, tx // 2
    corner_rows, own_rows = pl.ds(0, corner_half), pl.ds(corner_half, own_half)
    links = (
        (y1s, y1r, {fy_name: fy - 1}, pl.ds(0, half), 0),
        (ls, lr, {fx_name: fx - 1}, first_rows, 1),
        (ls, lr, {fx_name: fx - 1}, last_rows, 1),
        (rs, rr, {fx_name: fx + 1}, whole, 2),
        (y2s, y2r, {fy_name: fy + 1}, own_rows, 3),
        (y2s, y2r, {fy_name: fy + 1}, corner_rows, 3),
    )
    UP, LEFT_A, LEFT_B, RIGHT, DOWN_A, DOWN_B = range(6)

    def link(c, which):
        src, dst, where, rows, sent = links[which]
        return pltpu.make_async_remote_copy(
            src_ref=src.at[c, rows],
            dst_ref=dst.at[c, rows],
            send_sem=send_sem.at[sent],
            recv_sem=recv_sem.at[which, c],
            device_id=where,
            device_id_type=MESH,
        )

    def sent_all(which):
        src, dst, where, _, sent = links[which]
        return pltpu.make_async_remote_copy(
            src_ref=src,
            dst_ref=dst,
            send_sem=send_sem.at[sent],
            recv_sem=recv_sem.at[which, 0],
            device_id=where,
            device_id_type=MESH,
        )

    odd = lax.rem(fx, 2) == 1
    groups = n_fx // 2

    def turn(c, m):
        return ((c + 1) * m) // groups - (c * m) // groups == 1

    def leftward(which):
        return which != RIGHT

    def sends_via(c, which):
        if leftward(which):
            return jnp.logical_not(odd) & has_left & has_right & turn(c, fx // 2)
        return odd & has_left & has_right & jnp.logical_not(turn(c, (fx + 1) // 2))

    def to_via(c, which):
        src, _, _, rows, sent = links[which]
        return pltpu.make_async_remote_copy(
            src_ref=src.at[c, rows],
            dst_ref=via.at[c, rows],
            send_sem=send_sem.at[sent],
            recv_sem=via_recv.at[which, c],
            device_id={fx_name: fx + 1 if leftward(which) else fx - 1},
            device_id_type=MESH,
        )

    def passes_on(c, which):
        if leftward(which):
            return odd & (fx > 2) & turn(c, fx // 2)
        return jnp.logical_not(odd) & (fx < n_fx - 2) & jnp.logical_not(turn(c, (fx + 2) // 2))

    def from_via(c, which):
        _, dst, _, rows, _ = links[which]
        return pltpu.make_async_remote_copy(
            src_ref=via.at[c, rows],
            dst_ref=dst.at[c, rows],
            send_sem=via_send.at[which, c],
            recv_sem=recv_sem.at[which, c],
            device_id={fx_name: fx - 2 if leftward(which) else fx + 2},
            device_id_type=MESH,
        )

    def stage_via(ways, k):
        for j in range(n):
            c = k * n + j

            @pl.when(passes_on(c, ways[0]))
            def _(c=c):
                for way in ways:
                    to_via(c, way).wait_recv()
                    from_via(c, way).start()

    def to_side(c, which):
        around = sends_via(c, which)

        @pl.when(around)
        def _():
            to_via(c, which).start()

        @pl.when(jnp.logical_not(around))
        def _():
            link(c, which).start()

    load(0, 0).start()
    for i in range(4):
        constant(i).start()

    def loads(k, carry):
        load(k, 0).start()
        return carry

    def more_loads(k, carry):
        load(k, 1).start()
        load(k, 2).start()
        return carry

    lax.fori_loop(1, chunks, loads, 0)
    lax.fori_loop(0, chunks, more_loads, 0)
    for i in range(4, 9):
        constant(i).start()
    acc[...] = jnp.zeros_like(acc)

    peers = n_ch - 1
    for at, size in ((fy, n_fy), (fx, n_fx)):
        peers = peers + jnp.minimum(at, 1) + jnp.minimum(size - 1 - at, 1)
    peers = peers + jnp.minimum(fx // 2, 1) + jnp.minimum((n_fx - 1 - fx) // 2, 1)

    def lanes(rows):
        return lax.broadcasted_iota(jnp.int32, (rows, LANES), 1)

    def own_edge(rows):
        at = lanes(rows)
        return (at >= tail - border) & (at < tail)

    def roll(x, by):
        return pltpu.roll(x, by % LANES, 1)

    g = border // 3

    def pack_rest(rest, buffer, c):
        a, b, d = rest[:g], rest[g:2 * g], rest[2 * g:]
        low = lanes(g) < tail
        buffer[c, border:border + g] = jnp.where(low, a, roll(b, tail))
        buffer[c, border + g:] = jnp.where(low, d, roll(b, 2 * tail - LANES))

    def unpacked(buffer, c):
        p, q = buffer[c, border:border + g], buffer[c, border + g:]
        b = jnp.where(lanes(g) < LANES - tail, roll(p, -tail), roll(q, LANES - 2 * tail))
        return buffer[c, :border], jnp.concatenate([p, b, q], axis=0)

    half_lane = LANES // 2

    def stage_a(k):
        load(k, 0).wait()

        @pl.when(k == 0)
        def _():
            for i in range(4):
                constant(i).wait()

        x = dual[part(k)]
        hx, hy = ex // 2, ey // 2
        corner = corner_step(x[:, :hx, :hy], sy1_ref[...], sx1_ref[...])
        full = jnp.stack(
            [
                jnp.concatenate(
                    [jnp.concatenate([corner[j], x[j, :hx, hy:]], axis=1), x[j, hx:]], axis=0
                )
                for j in range(n)
            ]
        )
        mid = times_right(full, sy0_ref[...])
        for j in range(n):
            work[k * n + j] = times_left(sx0_ref[...], mid[j])

        @pl.when(k == 0)
        def _():
            pl.semaphore_wait(barrier, peers)

        @pl.when(has_up)
        def _():
            edge = own_edge(half)
            for j in range(n):
                c = k * n + j
                first, second = work[c, :half, LANES:], work[c, half:, LANES:]
                y1s[c] = jnp.where(edge, roll(first, -border), roll(second, half_lane - border))
                link(c, UP).start()

        @pl.when(has_left)
        def _():
            for j in range(n):
                c = k * n + j
                ls[c, :border] = work[c, :border, :LANES]
                to_side(c, LEFT_A)

    def stage_b(k):
        for j in range(n):
            c = k * n + j

            @pl.when(has_down)
            def _(c=c):
                link(c, UP).wait_recv()
                edge = own_edge(half)
                got = y1r[c]
                work[c, :half, LANES:] += jnp.where(edge, got, 0.0)
                work[c, half:, LANES:] += jnp.where(edge, roll(got, half_lane), 0.0)

            @pl.when(has_left)
            def _(c=c):
                pack_rest(work[c, :border, LANES:], ls, c)
                to_side(c, LEFT_B)

    def stage_c(k):
        load(k, 1).wait()
        load(k, 2).wait()
        xs = lax.broadcasted_iota(jnp.int32, (tx, ty), 0)
        ys = lax.broadcasted_iota(jnp.int32, (tx, ty), 1)
        ax = jnp.where((xs >= tx - border) & has_right, 0.5**0.5, 1.0).astype(F32)
        by = jnp.where((ys >= ty - border) & has_down, 0.5**0.5, 1.0).astype(F32)
        weight = ax * by
        for j in range(n):
            c = k * n + j

            @pl.when(has_right)
            def _(c=c):
                link(c, LEFT_A).wait_recv()
                link(c, LEFT_B).wait_recv()
                main, rest = unpacked(lr, c)
                work[c, ex - border:, :LANES] += main
                work[c, ex - border:, LANES:] += rest

            adjoint = work[c, border:, :ty] * weight
            current = image[c]
            fresh = jnp.maximum(current - TAU_STEP * (grad[c].astype(F32) + adjoint), 0.0)
            work[c, border:, :ty] = (2.0 * fresh - current) * weight
            next_ref[c] = fresh

            @pl.when(has_right)
            def _(c=c):
                rs[c, :border] = work[c, ex - border:, :LANES]
                pack_rest(work[c, ex - border:, LANES:], rs, c)
                to_side(c, RIGHT)

            @pl.when(has_down)
            def _(c=c):
                mid = border + own_half
                y2s[c, corner_half:] = jnp.where(
                    own_edge(own_half), work[c, border:mid, LANES:], roll(work[c, mid:, LANES:], half_lane)
                )
                link(c, DOWN_A).start()

    def stage_d(k):
        for j in range(n):
            c = k * n + j

            @pl.when(has_left)
            def _(c=c):
                link(c, RIGHT).wait_recv()
                main, rest = unpacked(rr, c)
                work[c, :border, :LANES] = main
                work[c, :border, LANES:] = rest

            @pl.when(jnp.logical_not(has_left))
            def _(c=c):
                work[c, :border] = jnp.zeros((border, ey), F32)

            @pl.when(has_down)
            def _(c=c):
                y2s[c, :corner_half] = jnp.where(
                    own_edge(corner_half),
                    work[c, :corner_half, LANES:],
                    roll(work[c, corner_half:border, LANES:], half_lane),
                )
                link(c, DOWN_B).start()

    def stage_e(k):
        @pl.when(k == 0)
        def _():
            for i in range(4, 8):
                constant(i).wait()

        for j in range(n):
            c = k * n + j
            for way in (LEFT_A, LEFT_B, RIGHT):
                @pl.when(passes_on(c, way))
                def _(c=c, way=way):
                    from_via(c, way).wait_send()

        @pl.when(has_up)
        def _():
            for j in range(n):
                c = k * n + j
                link(c, DOWN_A).wait_recv()
                link(c, DOWN_B).wait_recv()
                for at, rows, buffered in ((0, corner_half, 0), (border, own_half, corner_half)):
                    low = lanes(rows) < tail
                    got = y2r[c, buffered:buffered + rows]
                    first, second = pl.ds(at, rows), pl.ds(at + rows, rows)
                    work[c, first, LANES:] = jnp.where(low, work[c, first, LANES:], roll(got, border))
                    work[c, second, LANES:] = jnp.where(
                        low, work[c, second, LANES:], roll(got, border - half_lane)
                    )

        @pl.when(jnp.logical_not(has_up))
        def _():
            low = lanes(ex) < tail
            for j in range(n):
                c = k * n + j
                work[c, :, LANES:] = jnp.where(low, work[c, :, LANES:], 0.0)

        mid = times_right(work[part(k)], ay0_ref[...])
        hx, hy = ex // 2, ey // 2
        full = [times_left(ax0_ref[...], mid[j]) for j in range(n)]
        corner = corner_step(jnp.stack([f[:hx, :hy] for f in full]), ay1_ref[...], ax1_ref[...])
        total = acc[...]
        for j in range(n):
            c = k * n + j
            coeffs = jnp.concatenate(
                [jnp.concatenate([corner[j], full[j][:hx, hy:]], axis=1), full[j][hx:]], axis=0
            )
            updated = dual[c] + coeffs
            total = total + updated * updated
            upd_ref[c] = updated
        acc[...] = total

    stages = (
        (0, stage_a),
        (AT_B, stage_b),
        (AT_VIA_L, functools.partial(stage_via, (LEFT_A, LEFT_B))),
        (AT_VIA_R, functools.partial(stage_via, (RIGHT,))),
        (AT_C, stage_c),
        (AT_D, stage_d),
        (AT_E, stage_e),
    )

    def step(t, carry):
        for delay, stage in stages:
            @pl.when((t >= delay) & (t < chunks + delay))
            def _(delay=delay, stage=stage):
                stage(t - delay)
        return carry

    lax.fori_loop(0, chunks + AT_E, step, 0)

    def across(step):
        return pltpu.make_async_remote_copy(
            src_ref=acc,
            dst_ref=accr.at[step - 1],
            send_sem=ch_send.at[step - 1],
            recv_sem=ch_recv.at[step - 1],
            device_id={ch_name: lax.rem(ch + step, n_ch)},
            device_id_type=MESH,
        )

    for s in range(1, n_ch):
        across(s).start()
    for which, there in ((UP, has_up), (LEFT_A, has_left), (RIGHT, has_right), (DOWN_A, has_down)):
        @pl.when(there)
        def _(which=which):
            sent_all(which).wait_send()
    constant(8).wait()
    for s in range(1, n_ch):
        across(s).wait()
    total = acc[...]
    for s in range(1, n_ch):
        total = total + accr[s - 1]
    factor_ref[...] = jnp.minimum(1.0, LAMBDA_REG * rew_ref[...] / jnp.sqrt(total + EPSILON))


def shards(names, image_cube, data_grad, dual_coeffs, reweights):
    channels, tx, ty = image_cube.shape
    _, ex, ey = dual_coeffs.shape
    border = ex - tx
    n_ch = lax.axis_size(names[2])
    chunks = channels // CHUNK
    packed = border + 2 * (border // 3)
    wy0 = np.roll(level_matrix(ey), -(ey - ty), axis=1)
    wx0 = level_matrix(ex)
    wy1, wx1 = level_matrix(ey // 2), level_matrix(ex // 2)
    px0, px1 = round_up(ex, 16), round_up(ex // 2, 16)
    factors = (
        right_factor(wy0), left_factor(wx0.T, px0), right_factor(wy1), left_factor(wx1.T, px1),
        right_factor(wy0.T), left_factor(wx0, px0), right_factor(wy1.T), left_factor(wx1, px1),
    )
    far = pl.BlockSpec(memory_space=pltpu.HBM)
    inside = pl.BlockSpec(memory_space=pltpu.VMEM)
    lines = pltpu.VMEM((channels, ex // 2, LANES), F32)
    sides = pltpu.VMEM((channels, packed, LANES), F32)
    operands = (image_cube, data_grad, dual_coeffs, reweights, *factors)
    image_next, updated, factor = pl.pallas_call(
        functools.partial(kernel, names),
        out_shape=(
            pltpu.VMEM((channels, tx, ty), F32),
            pltpu.VMEM((channels, ex, ey), F32),
            pltpu.VMEM((ex, ey), F32),
        ),
        in_specs=[far] * len(operands),
        out_specs=(inside,) * 3,
        scratch_shapes=[
            *(pltpu.VMEM(f.shape, f.dtype) for f in factors),
            pltpu.VMEM((ex, ey), F32),
            pltpu.VMEM((channels, tx, ty), F32),
            pltpu.VMEM((channels, tx, ty), BF16),
            pltpu.VMEM((channels, ex, ey), F32),
            pltpu.VMEM((channels, ex, ey), F32),
            lines, lines, sides, sides, sides, sides, lines, lines, sides,
            pltpu.VMEM((ex, ey), F32),
            pltpu.VMEM((n_ch - 1, ex, ey), F32),
            pltpu.SemaphoreType.DMA((3, chunks)),
            pltpu.SemaphoreType.DMA((9,)),
            pltpu.SemaphoreType.DMA((4,)),
            pltpu.SemaphoreType.DMA((6, channels)),
            pltpu.SemaphoreType.DMA((4, channels)),
            pltpu.SemaphoreType.DMA((4, channels)),
            pltpu.SemaphoreType.DMA((n_ch - 1,)),
            pltpu.SemaphoreType.DMA((n_ch - 1,)),
        ],
        compiler_params=pltpu.CompilerParams(
            collective_id=0, has_side_effects=True, vmem_limit_bytes=40 * 2**20
        ),
        name="facets",
    )(*(pltpu.with_memory_space_constraint(a, pltpu.HBM) for a in operands))
    return image_next, updated * factor[None]


def solution(mesh):
    names = ("fy", "fx", "ch")
    return jax.shard_map(
        functools.partial(shards, names),
        mesh=mesh,
        in_specs=(P("ch", "fx", "fy"), P("ch", "fx", "fy"), P("ch", "fx", "fy"), P("fx", "fy")),
        out_specs=(P("ch", "fx", "fy"), P("ch", "fx", "fy")),
        check_vma=False,
    )
```

time: 79.8 us -> 74.7 us (0.936)
  Pallas kernels: 73.4 us -> 70.5 us
  other arithmetic: 4.28 us -> 2.11 us
    pallas_call x1, Pallas kernels: 73.4 us -> 70.5 us  [shards(): pl.pallas_call(functools.partial(kernel, names), out_shape=(pltpu.VMEM((c...]
    mul x1, other arithmetic: 4.28 us -> 2.11 us  [shards(): return (image_next, updated * factor[None])]
where the time goes in v1:
time: 74.7 us; the launch traced here: 74.5 us
  Pallas kernels  70.5 us (94%)
  other arithmetic  2.11 us (3%)
  local copies, waits for them, and re-layouts  1.32 us (2%)
    pallas_call x1, Pallas kernels, shards(): pl.pallas_call(functools.partial(kernel, names), out_shape=(pltpu.VMEM((c...  70.5 us
    mul x1, other arithmetic, shards(): return (image_next, updated * factor[None])  2.11 us

profile of v1, /device:TPU:19, one launch (start us, length us, event | category | flops | bytes accessed | tf_op | source)
XLA Modules:
  0.0 74.5 jit_solution(10997004556973314370)
XLA Ops:
  0.6 70.5 %facets.1 = (f32[32,64,208]{2,1,0:T(8,128)S(1)}, f32[32,112,256]{2,1,0:T(8,128)S(1)}, f32[112,256]{1,0:T(8,128)S(1)}) custom-call(f32[32,64,208]{2,1,0:T(8,128)} %image_hbm.1, bf16[32,64,208]{2,1,0:T(8,128)(2,1)} %grad_hbm.1, f32[32,112,256]{2,1,0:T(8,128)} %dual_hbm.1, f32[112,256]{1,0:T(8,128)} %rew_hbm.1, bf16[768,256]{1,0:T(8,128)(2,1)} %constant.16.clone.sy0_hbm, ...), custom_call_target="tpu_custom_call" | custom-call | tf_op jit(solution)/shard_map/facets/pallas_call | solution.py:550
  71.1 1.3 %copy.15 = f32[32,64,208]{2,1,0:T(8,128)} copy(f32[32,64,208]{2,1,0:T(8,128)S(1)} %get-tuple-element.8) | data formatting | bytes 3407872
  72.4 2.1 %broadcast_multiply_fusion = f32[32,112,256]{2,1,0:T(8,128)} fusion(f32[32,112,256]{2,1,0:T(8,128)S(1)} %get-tuple-element.6, f32[112,256]{1,0:T(8,128)S(1)} %get-tuple-element.7), kind=kLoop, calls=%fused_computation | loop fusion | flops 917504 | bytes 7454720 | tf_op jit(solution)/shard_map/mul | solution.py:583

commit v2 on v1

--- a/solution.py
+++ b/solution.py
@@ -31,8 +31,9 @@
 LAMBDA_REG = 1.0
 EPSILON = 1e-06
 LANES = 128
-CHUNK = 2
-AT_B, AT_VIA_L, AT_C, AT_VIA_R, AT_D, AT_E = 1, 2, 3, 5, 6, 8
+SUBLANES = 8
+CHUNK = 4
+AT_B, AT_VIA_L, AT_C, AT_VIA_R, AT_D, AT_E = 1, 2, 3, 4, 5, 6
 MESH = pl.DeviceIdType.MESH
 F32 = jnp.float32
 BF16 = jnp.bfloat16
@@ -106,14 +107,99 @@
     return pieces
 
 
+def lanes_of(rows):
+    return lax.broadcasted_iota(jnp.int32, (rows, LANES), 1)
+
+
+def roll(x, by):
+    return pltpu.roll(x, by % LANES, 1)
+
+
+def seats(border, tail):
+    groups = border // SUBLANES
+    bins = -(-groups * tail // LANES)
+    last = groups * tail - (bins - 1) * LANES
+    pieces, seat, at = [], 0, tail
+    for group in range(bins, groups):
+        lane = 0
+        while lane < tail:
+            room = LANES if seat < bins - 1 else last
+            if at == room:
+                seat, at = seat + 1, tail
+                continue
+            width = min(tail - lane, room - at)
+            pieces.append((group, lane, seat, at))
+            lane, at = lane + width, at + width
+    spare = LANES - last
+    kept = SUBLANES * last // LANES
+    folds = []
+    if spare:
+        assert last % spare == 0 and (SUBLANES - kept) * last == spare * kept
+        folds = [(row, (row - kept) * (last // spare)) for row in range(kept, SUBLANES)]
+    return groups, bins, last, kept, pieces, folds
+
+
+def packed_rows(border, tail):
+    _, bins, _, kept, _, _ = seats(border, tail)
+    return (bins - 1) * SUBLANES + kept
+
+
+def pack_rest(rest, tail, buffer, c, start):
+    groups, bins, last, kept, pieces, folds = seats(rest.shape[0], tail)
+    lane = lanes_of(SUBLANES)
+    row = lax.broadcasted_iota(jnp.int32, (SUBLANES, LANES), 0)
+    part = [rest[SUBLANES * i:SUBLANES * (i + 1)] for i in range(groups)]
+    out = part[:bins]
+    for group, source, seat, to in pieces:
+        out[seat] = jnp.where(lane >= to, roll(part[group], to - source), out[seat])
+    spare = LANES - last
+    end = out[-1]
+    for step in range(last // spare if folds else 0):
+        moved = roll(out[-1], last - spare * step)
+        for i, first in folds:
+            line = jnp.broadcast_to(moved[i:i + 1], (SUBLANES, LANES))
+            end = jnp.where((lane >= last) & (row == first + step), line, end)
+    for i in range(bins - 1):
+        buffer[c, start + SUBLANES * i:start + SUBLANES * (i + 1)] = out[i]
+    start += SUBLANES * (bins - 1)
+    buffer[c, start:start + kept] = end[:kept]
+
+
+def unpack_rest(buffer, c, start, border, tail):
+    groups, bins, last, kept, pieces, folds = seats(border, tail)
+    lane = lanes_of(SUBLANES)
+    row = lax.broadcasted_iota(jnp.int32, (SUBLANES, LANES), 0)
+    part = [buffer[c, start + SUBLANES * i:start + SUBLANES * (i + 1)] for i in range(bins - 1)]
+    start += SUBLANES * (bins - 1)
+    end = buffer[c, start:start + kept]
+    if folds:
+        end = jnp.concatenate([end, end[:SUBLANES - kept]], axis=0)
+    spare = LANES - last
+    whole = end
+    for step in range(last // spare if folds else 0):
+        moved = roll(end, spare * step - last)
+        for i, first in folds:
+            line = jnp.broadcast_to(moved[first + step:first + step + 1], (SUBLANES, LANES))
+            whole = jnp.where((lane >= step * spare) & (row == i), line, whole)
+    part.append(whole)
+    for group in range(bins, groups):
+        found = None
+        for owner, source, seat, to in pieces:
+            if owner == group:
+                moved = roll(part[seat], source - to)
+                found = moved if found is None else jnp.where(lane >= source, moved, found)
+        part.append(found)
+    return jnp.concatenate(part, axis=0)
+
+
 def kernel(
     names,
     image_hbm, grad_hbm, dual_hbm, rew_hbm,
     sy0_hbm, sx0_hbm, sy1_hbm, sx1_hbm, ay0_hbm, ax0_hbm, ay1_hbm, ax1_hbm,
     next_ref, upd_ref, factor_ref,
     sy0_ref, sx0_ref, sy1_ref, sx1_ref, ay0_ref, ax0_ref, ay1_ref, ax1_ref, rew_ref,
-    image, grad, dual, work, y1s, y1r, ls, lr, rs, rr, y2s, y2r, via, acc, accr,
-    in_sem, const_sem, send_sem, recv_sem, via_send, via_recv, ch_send, ch_recv,
+    image, grad, dual, work, weight, y1s, y1r, las, lar, lbs, lbr, rs, rr, y2s, y2r, acc, accr,
+    in_sem, const_sem, send_sem, recv_sem, side_recv, via_send, ch_send, ch_recv,
 ):
     fy_name, fx_name, ch_name = names
     channels, tx, ty = image.shape
@@ -123,7 +209,6 @@
     chunks = channels // n
     half = ex // 2
     tail = ty - LANES
-    packed = ls.shape[1]
     fy, fx, ch = (lax.axis_index(a) for a in names)
     n_fy, n_fx, n_ch = (lax.axis_size(a) for a in names)
     has_up, has_down = fy > 0, fy < n_fy - 1
@@ -164,36 +249,35 @@
         src, dst = constants[i]
         return pltpu.make_async_copy(src, dst, const_sem.at[i])
 
-    whole, first_rows, last_rows = pl.ds(0, packed), pl.ds(0, border), pl.ds(border, packed - border)
     corner_half, own_half = border // 2, tx // 2
     corner_rows, own_rows = pl.ds(0, corner_half), pl.ds(corner_half, own_half)
     links = (
-        (y1s, y1r, {fy_name: fy - 1}, pl.ds(0, half), 0),
-        (ls, lr, {fx_name: fx - 1}, first_rows, 1),
-        (ls, lr, {fx_name: fx - 1}, last_rows, 1),
-        (rs, rr, {fx_name: fx + 1}, whole, 2),
-        (y2s, y2r, {fy_name: fy + 1}, own_rows, 3),
-        (y2s, y2r, {fy_name: fy + 1}, corner_rows, 3),
+        (y1s, y1r, {fy_name: fy - 1}, None),
+        (y2s, y2r, {fy_name: fy + 1}, own_rows),
+        (y2s, y2r, {fy_name: fy + 1}, corner_rows),
     )
-    UP, LEFT_A, LEFT_B, RIGHT, DOWN_A, DOWN_B = range(6)
+    UP, DOWN_A, DOWN_B = range(3)
+    sides = ((las, lar), (lbs, lbr), (rs, rr))
+    LEFT_A, LEFT_B, RIGHT = range(3)
+    HERE, PASSING = 0, 1
 
     def link(c, which):
-        src, dst, where, rows, sent = links[which]
+        src, dst, where, rows = links[which]
         return pltpu.make_async_remote_copy(
-            src_ref=src.at[c, rows],
-            dst_ref=dst.at[c, rows],
-            send_sem=send_sem.at[sent],
+            src_ref=src.at[c] if rows is None else src.at[c, rows],
+            dst_ref=dst.at[c] if rows is None else dst.at[c, rows],
+            send_sem=send_sem.at[min(which, 1)],
             recv_sem=recv_sem.at[which, c],
             device_id=where,
             device_id_type=MESH,
         )
 
-    def sent_all(which):
-        src, dst, where, _, sent = links[which]
+    def link_sent(which):
+        src, dst, where, _ = links[which]
         return pltpu.make_async_remote_copy(
             src_ref=src,
             dst_ref=dst,
-            send_sem=send_sem.at[sent],
+            send_sem=send_sem.at[min(which, 1)],
             recv_sem=recv_sem.at[which, 0],
             device_id=where,
             device_id_type=MESH,
@@ -205,38 +289,60 @@
     def turn(c, m):
         return ((c + 1) * m) // groups - (c * m) // groups == 1
 
-    def leftward(which):
-        return which != RIGHT
-
     def sends_via(c, which):
-        if leftward(which):
+        if which != RIGHT:
             return jnp.logical_not(odd) & has_left & has_right & turn(c, fx // 2)
         return odd & has_left & has_right & jnp.logical_not(turn(c, (fx + 1) // 2))
 
-    def to_via(c, which):
-        src, _, _, rows, sent = links[which]
-        return pltpu.make_async_remote_copy(
-            src_ref=src.at[c, rows],
-            dst_ref=via.at[c, rows],
-            send_sem=send_sem.at[sent],
-            recv_sem=via_recv.at[which, c],
-            device_id={fx_name: fx + 1 if leftward(which) else fx - 1},
-            device_id_type=MESH,
-        )
-
     def passes_on(c, which):
-        if leftward(which):
+        if which != RIGHT:
             return odd & (fx > 2) & turn(c, fx // 2)
         return jnp.logical_not(odd) & (fx < n_fx - 2) & jnp.logical_not(turn(c, (fx + 2) // 2))
 
-    def from_via(c, which):
-        _, dst, _, rows, _ = links[which]
+    def to_side(c, which):
+        src, dst = sides[which]
+        ahead, back = (fx + 1, fx - 1) if which == RIGHT else (fx - 1, fx + 1)
+        around = sends_via(c, which)
+        slot = jnp.where(around, PASSING, HERE)
         return pltpu.make_async_remote_copy(
-            src_ref=via.at[c, rows],
-            dst_ref=dst.at[c, rows],
+            src_ref=src.at[c],
+            dst_ref=dst.at[slot, c],
+            send_sem=send_sem.at[2 + which],
+            recv_sem=side_recv.at[which, slot, c],
+            device_id={fx_name: jnp.where(around, back, ahead)},
+            device_id_type=MESH,
+        )
+
+    def side_sent(which):
+        src, dst = sides[which]
+        return pltpu.make_async_remote_copy(
+            src_ref=src,
+            dst_ref=dst.at[HERE],
+            send_sem=send_sem.at[2 + which],
+            recv_sem=side_recv.at[which, HERE, 0],
+            device_id={fx_name: fx + 1 if which == RIGHT else fx - 1},
+            device_id_type=MESH,
+        )
+
+    def arrival(c, which, slot):
+        src, dst = sides[which]
+        return pltpu.make_async_remote_copy(
+            src_ref=src.at[c],
+            dst_ref=dst.at[slot, c],
+            send_sem=send_sem.at[2 + which],
+            recv_sem=side_recv.at[which, slot, c],
+            device_id={fx_name: fx + 1 if which == RIGHT else fx - 1},
+            device_id_type=MESH,
+        )
+
+    def onward(c, which):
+        _, dst = sides[which]
+        return pltpu.make_async_remote_copy(
+            src_ref=dst.at[PASSING, c],
+            dst_ref=dst.at[HERE, c],
             send_sem=via_send.at[which, c],
-            recv_sem=recv_sem.at[which, c],
-            device_id={fx_name: fx - 2 if leftward(which) else fx + 2},
+            recv_sem=side_recv.at[which, HERE, c],
+            device_id={fx_name: fx + 2 if which == RIGHT else fx - 2},
             device_id_type=MESH,
         )
 
@@ -247,19 +353,8 @@
             @pl.when(passes_on(c, ways[0]))
             def _(c=c):
                 for way in ways:
-                    to_via(c, way).wait_recv()
-                    from_via(c, way).start()
-
-    def to_side(c, which):
-        around = sends_via(c, which)
-
-        @pl.when(around)
-        def _():
-            to_via(c, which).start()
-
-        @pl.when(jnp.logical_not(around))
-        def _():
-            link(c, which).start()
+                    arrival(c, way, PASSING).wait_recv()
+                    onward(c, way).start()
 
     load(0, 0).start()
     for i in range(4):
@@ -279,36 +374,25 @@
     for i in range(4, 9):
         constant(i).start()
     acc[...] = jnp.zeros_like(acc)
+    xs = lax.broadcasted_iota(jnp.int32, (tx, ty), 0)
+    ys = lax.broadcasted_iota(jnp.int32, (tx, ty), 1)
+    ax = jnp.where((xs >= tx - border) & has_right, 0.5**0.5, 1.0).astype(F32)
+    by = jnp.where((ys >= ty - border) & has_down, 0.5**0.5, 1.0).astype(F32)
+    weight[...] = ax * by
 
     peers = n_ch - 1
     for at, size in ((fy, n_fy), (fx, n_fx)):
         peers = peers + jnp.minimum(at, 1) + jnp.minimum(size - 1 - at, 1)
     peers = peers + jnp.minimum(fx // 2, 1) + jnp.minimum((n_fx - 1 - fx) // 2, 1)
 
-    def lanes(rows):
-        return lax.broadcasted_iota(jnp.int32, (rows, LANES), 1)
-
     def own_edge(rows):
-        at = lanes(rows)
+        at = lanes_of(rows)
         return (at >= tail - border) & (at < tail)
 
-    def roll(x, by):
-        return pltpu.roll(x, by % LANES, 1)
-
-    g = border // 3
-
-    def pack_rest(rest, buffer, c):
-        a, b, d = rest[:g], rest[g:2 * g], rest[2 * g:]
-        low = lanes(g) < tail
-        buffer[c, border:border + g] = jnp.where(low, a, roll(b, tail))
-        buffer[c, border + g:] = jnp.where(low, d, roll(b, 2 * tail - LANES))
-
-    def unpacked(buffer, c):
-        p, q = buffer[c, border:border + g], buffer[c, border + g:]
-        b = jnp.where(lanes(g) < LANES - tail, roll(p, -tail), roll(q, LANES - 2 * tail))
-        return buffer[c, :border], jnp.concatenate([p, b, q], axis=0)
-
     half_lane = LANES // 2
+
+    def members(k):
+        return [k * n + j for j in range(n)]
 
     def stage_a(k):
         load(k, 0).wait()
@@ -340,97 +424,100 @@
         @pl.when(has_up)
         def _():
             edge = own_edge(half)
-            for j in range(n):
-                c = k * n + j
+            for c in members(k):
                 first, second = work[c, :half, LANES:], work[c, half:, LANES:]
                 y1s[c] = jnp.where(edge, roll(first, -border), roll(second, half_lane - border))
+            for c in members(k):
                 link(c, UP).start()
 
         @pl.when(has_left)
         def _():
-            for j in range(n):
-                c = k * n + j
-                ls[c, :border] = work[c, :border, :LANES]
-                to_side(c, LEFT_A)
+            for c in members(k):
+                las[c] = work[c, :border, :LANES]
+            for c in members(k):
+                to_side(c, LEFT_A).start()
 
     def stage_b(k):
-        for j in range(n):
-            c = k * n + j
-
-            @pl.when(has_down)
-            def _(c=c):
+        @pl.when(has_down)
+        def _():
+            for c in members(k):
                 link(c, UP).wait_recv()
-                edge = own_edge(half)
+            edge = own_edge(half)
+            for c in members(k):
                 got = y1r[c]
                 work[c, :half, LANES:] += jnp.where(edge, got, 0.0)
                 work[c, half:, LANES:] += jnp.where(edge, roll(got, half_lane), 0.0)
 
-            @pl.when(has_left)
-            def _(c=c):
-                pack_rest(work[c, :border, LANES:], ls, c)
-                to_side(c, LEFT_B)
+        @pl.when(has_left)
+        def _():
+            for c in members(k):
+                pack_rest(work[c, :border, LANES:], tail, lbs, c, 0)
+            for c in members(k):
+                to_side(c, LEFT_B).start()
 
     def stage_c(k):
         load(k, 1).wait()
         load(k, 2).wait()
-        xs = lax.broadcasted_iota(jnp.int32, (tx, ty), 0)
-        ys = lax.broadcasted_iota(jnp.int32, (tx, ty), 1)
-        ax = jnp.where((xs >= tx - border) & has_right, 0.5**0.5, 1.0).astype(F32)
-        by = jnp.where((ys >= ty - border) & has_down, 0.5**0.5, 1.0).astype(F32)
-        weight = ax * by
-        for j in range(n):
-            c = k * n + j
-
-            @pl.when(has_right)
-            def _(c=c):
-                link(c, LEFT_A).wait_recv()
-                link(c, LEFT_B).wait_recv()
-                main, rest = unpacked(lr, c)
-                work[c, ex - border:, :LANES] += main
-                work[c, ex - border:, LANES:] += rest
-
-            adjoint = work[c, border:, :ty] * weight
+
+        @pl.when(has_right)
+        def _():
+            for c in members(k):
+                arrival(c, LEFT_A, HERE).wait_recv()
+                arrival(c, LEFT_B, HERE).wait_recv()
+            for c in members(k):
+                work[c, ex - border:, :LANES] += lar[HERE, c]
+                work[c, ex - border:, LANES:] += unpack_rest(lbr.at[HERE], c, 0, border, tail)
+
+        for c in members(k):
+            adjoint = work[c, border:, :ty] * weight[...]
             current = image[c]
             fresh = jnp.maximum(current - TAU_STEP * (grad[c].astype(F32) + adjoint), 0.0)
-            work[c, border:, :ty] = (2.0 * fresh - current) * weight
+            work[c, border:, :ty] = (2.0 * fresh - current) * weight[...]
             next_ref[c] = fresh
 
-            @pl.when(has_right)
-            def _(c=c):
+        @pl.when(has_right)
+        def _():
+            for c in members(k):
                 rs[c, :border] = work[c, ex - border:, :LANES]
-                pack_rest(work[c, ex - border:, LANES:], rs, c)
-                to_side(c, RIGHT)
-
-            @pl.when(has_down)
-            def _(c=c):
-                mid = border + own_half
+                pack_rest(work[c, ex - border:, LANES:], tail, rs, c, border)
+            for c in members(k):
+                to_side(c, RIGHT).start()
+
+        @pl.when(has_down)
+        def _():
+            mid = border + own_half
+            edge = own_edge(own_half)
+            for c in members(k):
                 y2s[c, corner_half:] = jnp.where(
-                    own_edge(own_half), work[c, border:mid, LANES:], roll(work[c, mid:, LANES:], half_lane)
+                    edge, work[c, border:mid, LANES:], roll(work[c, mid:, LANES:], half_lane)
                 )
+            for c in members(k):
                 link(c, DOWN_A).start()
 
     def stage_d(k):
-        for j in range(n):
-            c = k * n + j
-
-            @pl.when(has_left)
-            def _(c=c):
-                link(c, RIGHT).wait_recv()
-                main, rest = unpacked(rr, c)
-                work[c, :border, :LANES] = main
-                work[c, :border, LANES:] = rest
-
-            @pl.when(jnp.logical_not(has_left))
-            def _(c=c):
+        @pl.when(has_left)
+        def _():
+            for c in members(k):
+                arrival(c, RIGHT, HERE).wait_recv()
+            for c in members(k):
+                work[c, :border, :LANES] = rr[HERE, c, :border]
+                work[c, :border, LANES:] = unpack_rest(rr.at[HERE], c, border, border, tail)
+
+        @pl.when(jnp.logical_not(has_left))
+        def _():
+            for c in members(k):
                 work[c, :border] = jnp.zeros((border, ey), F32)
 
-            @pl.when(has_down)
-            def _(c=c):
+        @pl.when(has_down)
+        def _():
+            edge = own_edge(corner_half)
+            for c in members(k):
                 y2s[c, :corner_half] = jnp.where(
-                    own_edge(corner_half),
+                    edge,
                     work[c, :corner_half, LANES:],
                     roll(work[c, corner_half:border, LANES:], half_lane),
                 )
+            for c in members(k):
                 link(c, DOWN_B).start()
 
     def stage_e(k):
@@ -439,23 +526,16 @@
             for i in range(4, 8):
                 constant(i).wait()
 
-        for j in range(n):
-            c = k * n + j
-            for way in (LEFT_A, LEFT_B, RIGHT):
-                @pl.when(passes_on(c, way))
-                def _(c=c, way=way):
-                    from_via(c, way).wait_send()
-
         @pl.when(has_up)
         def _():
-            for j in range(n):
-                c = k * n + j
+            for c in members(k):
                 link(c, DOWN_A).wait_recv()
                 link(c, DOWN_B).wait_recv()
-                for at, rows, buffered in ((0, corner_half, 0), (border, own_half, corner_half)):
-                    low = lanes(rows) < tail
+            for at, rows, buffered in ((0, corner_half, 0), (border, own_half, corner_half)):
+                low = lanes_of(rows) < tail
+                first, second = pl.ds(at, rows), pl.ds(at + rows, rows)
+                for c in members(k):
                     got = y2r[c, buffered:buffered + rows]
-                    first, second = pl.ds(at, rows), pl.ds(at + rows, rows)
                     work[c, first, LANES:] = jnp.where(low, work[c, first, LANES:], roll(got, border))
                     work[c, second, LANES:] = jnp.where(
                         low, work[c, second, LANES:], roll(got, border - half_lane)
@@ -463,9 +543,8 @@
 
         @pl.when(jnp.logical_not(has_up))
         def _():
-            low = lanes(ex) < tail
-            for j in range(n):
-                c = k * n + j
+            low = lanes_of(ex) < tail
+            for c in members(k):
                 work[c, :, LANES:] = jnp.where(low, work[c, :, LANES:], 0.0)
 
         mid = times_right(work[part(k)], ay0_ref[...])
@@ -514,10 +593,24 @@
 
     for s in range(1, n_ch):
         across(s).start()
-    for which, there in ((UP, has_up), (LEFT_A, has_left), (RIGHT, has_right), (DOWN_A, has_down)):
+    for which, there in ((UP, has_up), (DOWN_A, has_down)):
         @pl.when(there)
         def _(which=which):
-            sent_all(which).wait_send()
+            link_sent(which).wait_send()
+    for which, there in ((LEFT_A, has_left), (LEFT_B, has_left), (RIGHT, has_right)):
+        @pl.when(there)
+        def _(which=which):
+            side_sent(which).wait_send()
+
+    def passed(c, carry):
+        for ways in ((LEFT_A, LEFT_B), (RIGHT,)):
+            @pl.when(passes_on(c, ways[0]))
+            def _(ways=ways):
+                for way in ways:
+                    onward(c, way).wait_send()
+        return carry
+
+    lax.fori_loop(0, channels, passed, 0)
     constant(8).wait()
     for s in range(1, n_ch):
         across(s).wait()
@@ -533,7 +626,7 @@
     border = ex - tx
     n_ch = lax.axis_size(names[2])
     chunks = channels // CHUNK
-    packed = border + 2 * (border // 3)
+    rest = packed_rows(border, ty - LANES)
     wy0 = np.roll(level_matrix(ey), -(ey - ty), axis=1)
     wx0 = level_matrix(ex)
     wy1, wx1 = level_matrix(ey // 2), level_matrix(ex // 2)
@@ -545,7 +638,12 @@
     far = pl.BlockSpec(memory_space=pltpu.HBM)
     inside = pl.BlockSpec(memory_space=pltpu.VMEM)
     lines = pltpu.VMEM((channels, ex // 2, LANES), F32)
-    sides = pltpu.VMEM((channels, packed, LANES), F32)
+    side_rows = (border, rest, border + rest)
+    side_bufs = [
+        pltpu.VMEM(shape, F32)
+        for rows in side_rows
+        for shape in ((channels, rows, LANES), (2, channels, rows, LANES))
+    ]
     operands = (image_cube, data_grad, dual_coeffs, reweights, *factors)
     image_next, updated, factor = pl.pallas_call(
         functools.partial(kernel, names),
@@ -563,15 +661,16 @@
             pltpu.VMEM((channels, tx, ty), BF16),
             pltpu.VMEM((channels, ex, ey), F32),
             pltpu.VMEM((channels, ex, ey), F32),
-            lines, lines, sides, sides, sides, sides, lines, lines, sides,
+            pltpu.VMEM((tx, ty), F32),
+            lines, lines, *side_bufs, lines, lines,
             pltpu.VMEM((ex, ey), F32),
             pltpu.VMEM((n_ch - 1, ex, ey), F32),
             pltpu.SemaphoreType.DMA((3, chunks)),
             pltpu.SemaphoreType.DMA((9,)),
-            pltpu.SemaphoreType.DMA((4,)),
-            pltpu.SemaphoreType.DMA((6, channels)),
-            pltpu.SemaphoreType.DMA((4, channels)),
-            pltpu.SemaphoreType.DMA((4, channels)),
+            pltpu.SemaphoreType.DMA((5,)),
+            pltpu.SemaphoreType.DMA((3, channels)),
+            pltpu.SemaphoreType.DMA((3, 2, channels)),
+            pltpu.SemaphoreType.DMA((3, channels)),
             pltpu.SemaphoreType.DMA((n_ch - 1,)),
             pltpu.SemaphoreType.DMA((n_ch - 1,)),
         ],

time: 74.7 us -> 72.1 us (0.965)
  Pallas kernels: 70.5 us -> 67.8 us
    pallas_call x1, Pallas kernels: 70.5 us -> 67.8 us  [shards(): pl.pallas_call(functools.partial(kernel, names), out_shape=(pltpu.VMEM((c...]
where the time goes in v2:
time: 72.1 us; the launch traced here: 71.9 us
  Pallas kernels  67.8 us (94%)
  other arithmetic  2.11 us (3%)
  local copies, waits for them, and re-layouts  1.32 us (2%)
    pallas_call x1, Pallas kernels, shards(): pl.pallas_call(functools.partial(kernel, names), out_shape=(pltpu.VMEM((c...  67.8 us
    mul x1, other arithmetic, shards(): return (image_next, updated * factor[None])  2.11 us

profile of v2, /device:TPU:19, one launch (start us, length us, event | category | flops | bytes accessed | tf_op | source)
XLA Modules:
  0.0 71.9 jit_solution(754124545623533625)
XLA Ops:
  0.6 67.8 %facets.1 = (f32[32,64,208]{2,1,0:T(8,128)S(1)}, f32[32,112,256]{2,1,0:T(8,128)S(1)}, f32[112,256]{1,0:T(8,128)S(1)}) custom-call(f32[32,64,208]{2,1,0:T(8,128)} %image_hbm.1, bf16[32,64,208]{2,1,0:T(8,128)(2,1)} %grad_hbm.1, f32[32,112,256]{2,1,0:T(8,128)} %dual_hbm.1, f32[112,256]{1,0:T(8,128)} %rew_hbm.1, bf16[768,256]{1,0:T(8,128)(2,1)} %constant.16.clone.sy0_hbm, ...), custom_call_target="tpu_custom_call" | custom-call | tf_op jit(solution)/shard_map/facets/pallas_call | solution.py:648
  68.5 1.3 %copy.15 = f32[32,64,208]{2,1,0:T(8,128)} copy(f32[32,64,208]{2,1,0:T(8,128)S(1)} %get-tuple-element.8) | data formatting | bytes 3407872
  69.8 2.1 %broadcast_multiply_fusion = f32[32,112,256]{2,1,0:T(8,128)} fusion(f32[32,112,256]{2,1,0:T(8,128)S(1)} %get-tuple-element.6, f32[112,256]{1,0:T(8,128)S(1)} %get-tuple-element.7), kind=kLoop, calls=%fused_computation | loop fusion | flops 917504 | bytes 7454720 | tf_op jit(solution)/shard_map/mul | solution.py:682

commit v3 on v2

--- a/solution.py
+++ b/solution.py
@@ -32,8 +32,9 @@
 EPSILON = 1e-06
 LANES = 128
 SUBLANES = 8
+PIECES = 8
 CHUNK = 4
-AT_B, AT_VIA_L, AT_C, AT_VIA_R, AT_D, AT_E = 1, 2, 3, 4, 5, 6
+AT_B, AT_VIA_L, AT_C, AT_VIA_R, AT_D, AT_E = 2, 3, 4, 7, 8, 9
 MESH = pl.DeviceIdType.MESH
 F32 = jnp.float32
 BF16 = jnp.bfloat16
@@ -394,11 +395,10 @@
     def members(k):
         return [k * n + j for j in range(n)]
 
-    def stage_a(k):
+    def stage_a(k, first=False):
         load(k, 0).wait()
 
-        @pl.when(k == 0)
-        def _():
+        if first:
             for i in range(4):
                 constant(i).wait()
 
@@ -417,8 +417,7 @@
         for j in range(n):
             work[k * n + j] = times_left(sx0_ref[...], mid[j])
 
-        @pl.when(k == 0)
-        def _():
+        if first:
             pl.semaphore_wait(barrier, peers)
 
         @pl.when(has_up)
@@ -564,22 +563,26 @@
 
     stages = (
         (0, stage_a),
-        (AT_B, stage_b),
-        (AT_VIA_L, functools.partial(stage_via, (LEFT_A, LEFT_B))),
-        (AT_VIA_R, functools.partial(stage_via, (RIGHT,))),
-        (AT_C, stage_c),
-        (AT_D, stage_d),
-        (AT_E, stage_e),
+        (1, stage_b),
+        (2, functools.partial(stage_via, (LEFT_A, LEFT_B))),
+        (3, stage_c),
+        (4, functools.partial(stage_via, (RIGHT,))),
+        (5, stage_d),
+        (6, stage_e),
     )
+
+    stage_a(0, True)
 
     def step(t, carry):
         for delay, stage in stages:
-            @pl.when((t >= delay) & (t < chunks + delay))
+            early = 1 if stage is stage_a else 0
+
+            @pl.when((t >= delay + early) & (t < chunks + delay))
             def _(delay=delay, stage=stage):
                 stage(t - delay)
         return carry
 
-    lax.fori_loop(0, chunks + AT_E, step, 0)
+    lax.fori_loop(0, chunks + 6, step, 0)
 
     def across(step):
         return pltpu.make_async_remote_copy(
@@ -618,6 +621,33 @@
     for s in range(1, n_ch):
         total = total + accr[s - 1]
     factor_ref[...] = jnp.minimum(1.0, LAMBDA_REG * rew_ref[...] / jnp.sqrt(total + EPSILON))
+
+
+def finish(image_ref, upd_ref, factor_ref, next_hbm, dual_hbm, scaled, sem):
+    channels = upd_ref.shape[0]
+    n = channels // PIECES
+
+    def image_out(i):
+        at = pl.ds(i * n, n)
+        return pltpu.make_async_copy(image_ref.at[at], next_hbm.at[at], sem.at[0, i])
+
+    def dual_out(i):
+        at = pl.ds(i * n, n)
+        return pltpu.make_async_copy(scaled.at[at], dual_hbm.at[at], sem.at[1, i])
+
+    for i in range(PIECES):
+        image_out(i).start()
+
+    def piece(i, carry):
+        for j in range(n):
+            scaled[i * n + j] = upd_ref[i * n + j] * factor_ref[...]
+        dual_out(i).start()
+        return carry
+
+    lax.fori_loop(0, PIECES, piece, 0)
+    for i in range(PIECES):
+        image_out(i).wait()
+        dual_out(i).wait()
 
 
 def shards(names, image_cube, data_grad, dual_coeffs, reweights):
@@ -679,7 +709,22 @@
         ),
         name="facets",
     )(*(pltpu.with_memory_space_constraint(a, pltpu.HBM) for a in operands))
-    return image_next, updated * factor[None]
+    anywhere = pl.BlockSpec(memory_space=pl.ANY)
+    return pl.pallas_call(
+        finish,
+        out_shape=(
+            jax.ShapeDtypeStruct((channels, tx, ty), F32),
+            jax.ShapeDtypeStruct((channels, ex, ey), F32),
+        ),
+        in_specs=[inside] * 3,
+        out_specs=(anywhere, anywhere),
+        scratch_shapes=[
+            pltpu.VMEM((channels, ex, ey), F32),
+            pltpu.SemaphoreType.DMA((2, PIECES)),
+        ],
+        compiler_params=pltpu.CompilerParams(vmem_limit_bytes=40 * 2**20),
+        name="finish",
+    )(*(pltpu.with_memory_space_constraint(a, pltpu.VMEM) for a in (image_next, updated, factor)))
 
 
 def solution(mesh):

time: 72.1 us -> 71.1 us (0.986); the launches traced: 71.9 us -> 70.1 us
  other arithmetic: 2.11 us -> 0 us
  Pallas kernels: 67.8 us -> 69.5 us
  local copies, waits for them, and re-layouts: 1.32 us -> 0 us
    pallas_call x0 -> x1, Pallas kernels: none -> 2.63 us  [shards(): pl.pallas_call(finish, out_shape=(jax.ShapeDtypeStruct((channels, tx, ty)...]
    mul x1 -> x0, other arithmetic: 2.11 us -> none  [shards(): return (image_next, updated * factor[None])]
    unnamed x1 -> x0, local copies, waits for them, and re-layouts: 1.32 us -> none
    pallas_call x1, Pallas kernels: 67.8 us -> 66.8 us  [shards(): pl.pallas_call(functools.partial(kernel, names), out_shape=(pltpu.VMEM((c...]
where the time goes in v3:
time: 71.1 us; the launch traced here: 70.1 us
  Pallas kernels  69.5 us (98%)
    pallas_call x1, Pallas kernels, shards(): pl.pallas_call(functools.partial(kernel, names), out_shape=(pltpu.VMEM((c...  66.8 us
    pallas_call x1, Pallas kernels, shards(): pl.pallas_call(finish, out_shape=(jax.ShapeDtypeStruct((channels, tx, ty)...  2.63 us

profile of v3, /device:TPU:19, one launch (start us, length us, event | category | flops | bytes accessed | tf_op | source)
XLA Modules:
  0.0 70.1 jit_solution(6779246669742913837)
XLA Ops:
  0.6 66.8 %facets.1 = (f32[32,64,208]{2,1,0:T(8,128)S(1)}, f32[32,112,256]{2,1,0:T(8,128)S(1)}, f32[112,256]{1,0:T(8,128)S(1)}) custom-call(f32[32,64,208]{2,1,0:T(8,128)} %image_hbm.1, bf16[32,64,208]{2,1,0:T(8,128)(2,1)} %grad_hbm.1, f32[32,112,256]{2,1,0:T(8,128)} %dual_hbm.1, f32[112,256]{1,0:T(8,128)} %rew_hbm.1, bf16[768,256]{1,0:T(8,128)(2,1)} %constant.16.clone.sy0_hbm, ...), custom_call_target="tpu_custom_call" | custom-call | tf_op jit(solution)/shard_map/facets/pallas_call | solution.py:678
  67.5 2.6 %finish.1 = (f32[32,64,208]{2,1,0:T(8,128)}, f32[32,112,256]{2,1,0:T(8,128)}) custom-call(f32[32,64,208]{2,1,0:T(8,128)S(1)} %get-tuple-element.5.image_ref, f32[32,112,256]{2,1,0:T(8,128)S(1)} %get-tuple-element.6.upd_ref, f32[112,256]{1,0:T(8,128)S(1)} %get-tuple-element.7.factor_ref), custom_call_target="tpu_custom_call" | custom-call | tf_op jit(solution)/shard_map/finish/pallas_call | solution.py:713

commit v4 on v3

--- a/solution.py
+++ b/solution.py
@@ -33,6 +33,7 @@
 LANES = 128
 SUBLANES = 8
 PIECES = 8
+SUB = 2
 CHUNK = 4
 AT_B, AT_VIA_L, AT_C, AT_VIA_R, AT_D, AT_E = 2, 3, 4, 7, 8, 9
 MESH = pl.DeviceIdType.MESH
@@ -370,10 +371,12 @@
         load(k, 2).start()
         return carry
 
-    lax.fori_loop(1, chunks, loads, 0)
-    lax.fori_loop(0, chunks, more_loads, 0)
-    for i in range(4, 9):
-        constant(i).start()
+    def load_others():
+        lax.fori_loop(1, chunks, loads, 0)
+        for i in range(4, 9):
+            constant(i).start()
+        lax.fori_loop(0, chunks, more_loads, 0)
+
     acc[...] = jnp.zeros_like(acc)
     xs = lax.broadcasted_iota(jnp.int32, (tx, ty), 0)
     ys = lax.broadcasted_iota(jnp.int32, (tx, ty), 1)
@@ -401,6 +404,7 @@
         if first:
             for i in range(4):
                 constant(i).wait()
+            load_others()
 
         x = dual[part(k)]
         hx, hy = ex // 2, ey // 2
@@ -493,31 +497,35 @@
             for c in members(k):
                 link(c, DOWN_A).start()
 
-    def stage_d(k):
+    def part_d(some):
         @pl.when(has_left)
         def _():
-            for c in members(k):
+            for c in some:
                 arrival(c, RIGHT, HERE).wait_recv()
-            for c in members(k):
+            for c in some:
                 work[c, :border, :LANES] = rr[HERE, c, :border]
                 work[c, :border, LANES:] = unpack_rest(rr.at[HERE], c, border, border, tail)
 
         @pl.when(jnp.logical_not(has_left))
         def _():
-            for c in members(k):
+            for c in some:
                 work[c, :border] = jnp.zeros((border, ey), F32)
 
         @pl.when(has_down)
         def _():
             edge = own_edge(corner_half)
-            for c in members(k):
+            for c in some:
                 y2s[c, :corner_half] = jnp.where(
                     edge,
                     work[c, :corner_half, LANES:],
                     roll(work[c, corner_half:border, LANES:], half_lane),
                 )
-            for c in members(k):
+            for c in some:
                 link(c, DOWN_B).start()
+
+    def stage_d(k):
+        for j in range(0, n, SUB):
+            part_d(members(k)[j:j + SUB])
 
     def stage_e(k):
         @pl.when(k == 0)

time: 71.1 us -> 70.8 us (level)
  no operation moved by 1% of the time
where the time goes in v4:
time: 70.8 us; the launch traced here: 70.2 us
  Pallas kernels  69.5 us (98%)
    pallas_call x1, Pallas kernels, shards(): pl.pallas_call(functools.partial(kernel, names), out_shape=(pltpu.VMEM((c...  66.9 us
    pallas_call x1, Pallas kernels, shards(): pl.pallas_call(finish, out_shape=(jax.ShapeDtypeStruct((channels, tx, ty)...  2.63 us

profile of v4, /device:TPU:19, one launch (start us, length us, event | category | flops | bytes accessed | tf_op | source)
XLA Modules:
  0.0 70.2 jit_solution(16076188406469728029)
XLA Ops:
  0.6 66.9 %facets.1 = (f32[32,64,208]{2,1,0:T(8,128)S(1)}, f32[32,112,256]{2,1,0:T(8,128)S(1)}, f32[112,256]{1,0:T(8,128)S(1)}) custom-call(f32[32,64,208]{2,1,0:T(8,128)} %image_hbm.1, bf16[32,64,208]{2,1,0:T(8,128)(2,1)} %grad_hbm.1, f32[32,112,256]{2,1,0:T(8,128)} %dual_hbm.1, f32[112,256]{1,0:T(8,128)} %rew_hbm.1, bf16[768,256]{1,0:T(8,128)(2,1)} %constant.16.clone.sy0_hbm, ...), custom_call_target="tpu_custom_call" | custom-call | tf_op jit(solution)/shard_map/facets/pallas_call | solution.py:686
  67.5 2.6 %finish.1 = (f32[32,64,208]{2,1,0:T(8,128)}, f32[32,112,256]{2,1,0:T(8,128)}) custom-call(f32[32,64,208]{2,1,0:T(8,128)S(1)} %get-tuple-element.5.image_ref, f32[32,112,256]{2,1,0:T(8,128)S(1)} %get-tuple-element.6.upd_ref, f32[112,256]{1,0:T(8,128)S(1)} %get-tuple-element.7.factor_ref), custom_call_target="tpu_custom_call" | custom-call | tf_op jit(solution)/shard_map/finish/pallas_call | solution.py:721

commit v5 on v4

--- a/solution.py
+++ b/solution.py
@@ -288,18 +288,15 @@
     odd = lax.rem(fx, 2) == 1
     groups = n_fx // 2
 
-    def turn(c, m):
-        return ((c + 1) * m) // groups - (c * m) // groups == 1
-
     def sends_via(c, which):
         if which != RIGHT:
-            return jnp.logical_not(odd) & has_left & has_right & turn(c, fx // 2)
-        return odd & has_left & has_right & jnp.logical_not(turn(c, (fx + 1) // 2))
+            return jnp.logical_not(odd) & has_left & has_right & (lax.rem(c, groups) >= groups - fx // 2)
+        return odd & has_left & has_right & (lax.rem(c, groups) >= (fx + 1) // 2)
 
     def passes_on(c, which):
         if which != RIGHT:
-            return odd & (fx > 2) & turn(c, fx // 2)
-        return jnp.logical_not(odd) & (fx < n_fx - 2) & jnp.logical_not(turn(c, (fx + 2) // 2))
+            return odd & (fx > 2) & (lax.rem(c, groups) >= groups - fx // 2)
+        return jnp.logical_not(odd) & (fx < n_fx - 2) & (lax.rem(c, groups) >= (fx + 2) // 2)
 
     def to_side(c, which):
         src, dst = sides[which]

time: 70.8 us -> 70.5 us (level)
  no operation moved by 1% of the time
where the time goes in v5:
time: 70.5 us; the launch traced here: 70.1 us
  Pallas kernels  69.5 us (99%)
    pallas_call x1, Pallas kernels, shards(): pl.pallas_call(functools.partial(kernel, names), out_shape=(pltpu.VMEM((c...  66.9 us
    pallas_call x1, Pallas kernels, shards(): pl.pallas_call(finish, out_shape=(jax.ShapeDtypeStruct((channels, tx, ty)...  2.63 us

profile of v5, /device:TPU:19, one launch (start us, length us, event | category | flops | bytes accessed | tf_op | source)
XLA Modules:
  0.0 70.1 jit_solution(9154745311282378017)
XLA Ops:
  0.6 66.9 %facets.1 = (f32[32,64,208]{2,1,0:T(8,128)S(1)}, f32[32,112,256]{2,1,0:T(8,128)S(1)}, f32[112,256]{1,0:T(8,128)S(1)}) custom-call(f32[32,64,208]{2,1,0:T(8,128)} %image_hbm.1, bf16[32,64,208]{2,1,0:T(8,128)(2,1)} %grad_hbm.1, f32[32,112,256]{2,1,0:T(8,128)} %dual_hbm.1, f32[112,256]{1,0:T(8,128)} %rew_hbm.1, bf16[768,256]{1,0:T(8,128)(2,1)} %constant.16.clone.sy0_hbm, ...), custom_call_target="tpu_custom_call" | custom-call | tf_op jit(solution)/shard_map/facets/pallas_call | solution.py:683
  67.5 2.6 %finish.1 = (f32[32,64,208]{2,1,0:T(8,128)}, f32[32,112,256]{2,1,0:T(8,128)}) custom-call(f32[32,64,208]{2,1,0:T(8,128)S(1)} %get-tuple-element.5.image_ref, f32[32,112,256]{2,1,0:T(8,128)S(1)} %get-tuple-element.6.upd_ref, f32[112,256]{1,0:T(8,128)S(1)} %get-tuple-element.7.factor_ref), custom_call_target="tpu_custom_call" | custom-call | tf_op jit(solution)/shard_map/finish/pallas_call | solution.py:718
